TPU v7x, 32 devices: a whole 2x2x4 slice. The times are simulated.
32 devices in a mesh: slices: 2 (over x), wide: 4 (over y, core), narrow: 4 (over z).
Axes of the slice: x: 2, y: 2, z: 4, core: 2. Of those that a mesh axis runs over, the one named last changes fastest.
Arguments:
- state: float32 [8, 4, 2, 16384], P(('slices', 'wide'), 'narrow'), parts along dimension 0, may hold values from -6 to 6
- gates: float32 [8, 7, 2, 4, 4], replicated, may hold values from -2 to 2
Outputs:
- final_state: float32 [8, 4, 2, 16384], P(('slices', 'wide'), 'narrow'), parts along dimension 0
- marginal: float32 [8, 16384], P(('slices', 'wide'), 'narrow'), parts along dimension 0
There are 2 independent parts, one for each index of `slices`. A program takes and returns all parts, laid end to end along the dimension named above; an argument that names none is the same for every part. Nothing has to cross between parts.
All inputs are finite; a program needn't handle non-finite values.
Results may differ from a plain program's by a relative error of at most 0.0003.
Values sent between devices are 32-bit elements; how exact they have to be, the bound alone decides.
A program may use at most 192 MiB of HBM per device.

v0:
```python
import functools

import jax
import jax.numpy as jnp
from jax import lax
from jax.experimental import pallas as pl
from jax.experimental.pallas import tpu as pltpu
from jax.sharding import PartitionSpec as P


def kron_chain(members):
    real_part = members[0][0]
    imag_part = members[0][1]
    for member in members[1:]:
        other_real = member[0]
        other_imag = member[1]
        new_real = jnp.kron(real_part, other_real) - jnp.kron(imag_part, other_imag)
        new_imag = jnp.kron(real_part, other_imag) + jnp.kron(imag_part, other_real)
        real_part, imag_part = (new_real, new_imag)
    return (real_part, imag_part)


def rotate(flat, wide_count, narrow_count):
    devices = wide_count * narrow_count
    amplitudes = flat.shape[1]
    rest = amplitudes // devices
    blocks = flat.reshape(2, rest, devices)
    turned = jnp.swapaxes(blocks, 1, 2)
    moved = lax.all_to_all(turned, ("wide", "narrow"), split_axis=1, concat_axis=1, tiled=True)
    return moved.reshape(2, amplitudes)


def apply_layer(flat, layer_gates):
    amplitudes = flat.shape[1]
    pairs = layer_gates.shape[0]
    upper = amplitudes // 256
    low_real, low_imag = kron_chain([layer_gates[index] for index in range(3, -1, -1)])
    high_real, high_imag = kron_chain([layer_gates[index] for index in range(pairs - 1, 3, -1)])
    blocks = flat.reshape(2, upper, 256)
    real_rows = blocks[0]
    imag_rows = blocks[1]
    highest = lax.Precision.HIGHEST
    next_real = jnp.dot(real_rows, low_real.T, precision=highest) - jnp.dot(
        imag_rows, low_imag.T, precision=highest
    )
    next_imag = jnp.dot(real_rows, low_imag.T, precision=highest) + jnp.dot(
        imag_rows, low_real.T, precision=highest
    )
    final_real = jnp.dot(high_real, next_real, precision=highest) - jnp.dot(
        high_imag, next_imag, precision=highest
    )
    final_imag = jnp.dot(high_imag, next_real, precision=highest) + jnp.dot(
        high_real, next_imag, precision=highest
    )
    return jnp.stack([final_real, final_imag]).reshape(2, amplitudes)


MESH = pl.DeviceIdType.MESH
LANES = 128


def complex_mul(left, right):
    return (
        left[0] * right[0] - left[1] * right[1],
        left[0] * right[1] + left[1] * right[0],
    )


def small_matmul(left, right):
    total = None
    for index in range(right[0].shape[0]):
        column = tuple(part[:, index : index + 1] for part in left)
        row = tuple(part[index : index + 1, :] for part in right)
        term = complex_mul(column, row)
        total = term if total is None else tuple(a + b for a, b in zip(total, term))
    return total


def merged_gate(gate_ref, layers, pairs, shift, total_pairs, which):
    product = None
    for layer in range(layers):
        index = (which - layer * shift) % total_pairs
        if index < pairs:
            at = (layer * pairs + index) * 2
            gate = (gate_ref[at], gate_ref[at + 1])
            product = gate if product is None else small_matmul(gate, product)
    return product


def kron_all(members):
    radix = members[0][0].shape[0]
    size = radix ** len(members)
    lane = lax.broadcasted_iota(jnp.int32, (1, size), 1)
    rows = None
    for place, member in enumerate(reversed(members)):
        field = (lane // radix**place) % radix
        wide = []
        for part in member:
            spread = jnp.broadcast_to(part[:, radix - 1 : radix], (radix, size))
            for index in range(radix - 1):
                spread = jnp.where(field == index, part[:, index : index + 1], spread)
            wide.append(spread)
        if rows is None:
            rows = tuple(wide)
            continue
        pieces = [
            complex_mul(tuple(part[index : index + 1, :] for part in wide), rows)
            for index in range(radix)
        ]
        rows = tuple(jnp.concatenate([piece[c] for piece in pieces], axis=0) for c in range(2))
    return rows


def split(value):
    high = value.astype(jnp.bfloat16)
    return high, (value - high.astype(jnp.float32)).astype(jnp.bfloat16)


def dot_t(left, right):
    def one(a, b):
        return lax.dot_general(a, b, (((1,), (1,)), ((), ())), preferred_element_type=jnp.float32)

    return one(left[0], right[0]) + (one(left[0], right[1]) + one(left[1], right[0]))


def window_kernel(plan, x_hbm, g_hbm, out_hbm, marg_hbm, x, g, send, recv, fin, prob, part, marg,
                  local_sem, send_sem, recv_sem, psend_sem, precv_sem):
    layers, pairs, shift, total_pairs, start, radix = plan
    w = lax.axis_index("wide")
    n = lax.axis_index("narrow")
    offsets = [(dw, dn) for dw in range(radix) for dn in range(radix) if dw or dn]

    def partner(dw, dn):
        return lax.rem(w + dw, radix), lax.rem(n + dn, radix)

    barrier = pltpu.get_barrier_semaphore()
    for dw, dn in offsets:
        pw, pn = partner(dw, dn)
        pl.semaphore_signal(barrier, inc=1, device_id={"wide": pw, "narrow": pn}, device_id_type=MESH)
    copy_g = pltpu.make_async_copy(g_hbm, g, local_sem.at[0])
    copy_x = pltpu.make_async_copy(x_hbm, x, local_sem.at[1])
    copy_g.start()
    copy_x.start()
    copy_g.wait()

    gate_of = functools.partial(merged_gate, g, layers, pairs, shift, total_pairs)
    low_gate = gate_of(start)
    high_gate = gate_of(start + 1)

    half = LANES // 2
    rows_hi = send.shape[1]
    lane = lax.broadcasted_iota(jnp.int32, (rows_hi, LANES), 1)
    first = lane < half
    shape = (rows_hi, LANES)

    def entry(gate, row, column):
        return tuple(
            jnp.broadcast_to(part_[row : row + 1, column : column + 1], shape) for part_ in gate
        )

    def both(gate, one, other):
        return tuple(jnp.where(first, a, b) for a, b in zip(entry(gate, *one), entry(gate, *other)))

    def add(total, term):
        return term if total is None else (total[0] + term[0], total[1] + term[1])

    copy_x.wait()
    same = [[both(low_gate, (2 * o, 2 * i), (2 * o + 1, 2 * i + 1)) for i in range(2)] for o in range(2)]
    cross = [[both(low_gate, (2 * o, 2 * i + 1), (2 * o + 1, 2 * i)) for i in range(2)] for o in range(2)]
    stage = []
    stride = 4 * radix
    for high in range(radix):
        held = []
        for i in range(2):
            held.append(tuple(x[pl.ds(high * 4 + i * 2 + c, rows_hi, stride=stride), :] for c in range(2)))
        turned = [tuple(pltpu.roll(v, half, 1) for v in pair) for pair in held]
        result = []
        for o in range(2):
            total = None
            for i in range(2):
                total = add(total, complex_mul(same[o][i], held[i]))
                total = add(total, complex_mul(cross[o][i], turned[i]))
            result.append(total)
        stage.append(result)
    for out_high in range(radix):
        coefs = [entry(high_gate, out_high, high) for high in range(radix)]
        for o in range(2):
            total = None
            for high in range(radix):
                total = add(total, complex_mul(coefs[high], stage[high][o]))
            rolled = tuple(pltpu.roll(v, half, 1) for v in total)
            send[out_high * radix + 2 * o] = jnp.where(first, total[0], rolled[1])
            send[out_high * radix + 2 * o + 1] = jnp.where(first, rolled[0], total[1])

    pl.semaphore_wait(barrier, len(offsets))
    me = w * radix + n
    copies = []
    for at, (dw, dn) in enumerate(offsets):
        pw, pn = partner(dw, dn)
        copy = pltpu.make_async_remote_copy(
            src_ref=send.at[pw * radix + pn],
            dst_ref=recv.at[me],
            send_sem=send_sem.at[at],
            recv_sem=recv_sem.at[at],
            device_id={"wide": pw, "narrow": pn},
            device_id_type=MESH,
        )
        copy.start()
        copies.append(copy)
    recv[me] = send[me]

    low = kron_all([gate_of(which) for which in range(start - 1, -1, -1)])
    lane_form = split(
        jnp.concatenate(
            [
                jnp.concatenate([low[0], -low[1]], axis=1),
                jnp.concatenate([low[1], low[0]], axis=1),
            ],
            axis=0,
        )
    )
    row_real, row_imag = kron_all([gate_of(which) for which in range(total_pairs - 1, start + 1, -1)])
    row_real = split(row_real)
    row_imag = split(row_imag)

    for copy in copies:
        copy.wait_recv()
    count = radix * radix
    size = count * rows_hi
    turned = split(dot_t(lane_form, split(recv[...].reshape(size, LANES))))
    with_real = dot_t(turned, row_real)
    with_imag = dot_t(turned, row_imag)
    real = with_real[:half] - with_imag[half:]
    imag = with_real[half:] + with_imag[:half]
    density = real * real + imag * imag
    own_rows = half // radix
    for index in range(radix):
        prob[index] = density[index * own_rows : (index + 1) * own_rows]
    blocks = size // LANES
    for block in range(blocks):
        columns = slice(block * LANES, (block + 1) * LANES)
        fin[pl.ds(block * 2, half, stride=2 * blocks), :] = real[:, columns]
        fin[pl.ds(block * 2 + 1, half, stride=2 * blocks), :] = imag[:, columns]
    sums = []
    for dn in range(1, radix):
        pn = lax.rem(n + dn, radix)
        copy = pltpu.make_async_remote_copy(
            src_ref=prob.at[pn],
            dst_ref=part.at[dn - 1],
            send_sem=psend_sem.at[dn - 1],
            recv_sem=precv_sem.at[dn - 1],
            device_id={"wide": w, "narrow": pn},
            device_id_type=MESH,
        )
        copy.start()
        sums.append(copy)
    out_copy = pltpu.make_async_copy(fin, out_hbm, local_sem.at[0])
    out_copy.start()
    for copy in copies:
        copy.wait_send()
    total = prob[n]
    for index, copy in enumerate(sums):
        copy.wait_recv()
        total = total + part[index]
    for block in range(blocks):
        marg[pl.ds(block, own_rows, stride=blocks), :] = total[:, block * LANES : (block + 1) * LANES]
    marg_copy = pltpu.make_async_copy(marg, marg_hbm, local_sem.at[1])
    marg_copy.start()
    for copy in sums:
        copy.wait_send()
    out_copy.wait()
    marg_copy.wait()


def window_plan(wide_count, narrow_count, amplitudes, gates_shape):
    layers, pairs, radix = gates_shape[0], gates_shape[1], gates_shape[-1]
    high_bits = (wide_count * narrow_count).bit_length() - 1
    local_bits = amplitudes.bit_length() - 1
    total_bits = high_bits + local_bits
    if high_bits % 2 or local_bits % 2 or wide_count != radix or narrow_count != radix:
        return None
    if 2 * pairs != local_bits:
        return None
    offset = ((layers - 1) * high_bits) % total_bits
    start = offset // 2 - high_bits // 2
    if start < 1 or offset // 2 >= pairs or 2 * radix**start != LANES:
        return None
    rows_hi = radix ** (pairs - offset // 2)
    if rows_hi % 8:
        return None
    for which in range(total_bits // 2):
        if all((which - layer * (high_bits // 2)) % (total_bits // 2) >= pairs for layer in range(layers)):
            return None
    return (layers, pairs, high_bits // 2, total_bits // 2, start, radix), rows_hi


def merged_local(plan, rows_hi, state, gates):
    radix = plan[-1]
    amplitudes = state.shape[-1]
    rows = amplitudes // LANES
    count = radix * radix
    own = amplitudes // radix // LANES
    x = jnp.swapaxes(state.reshape(2, rows, LANES), 0, 1).reshape(2 * rows, LANES)
    g = gates.reshape(-1, radix, radix)
    f32 = jnp.float32
    wide_lanes = count * rows_hi
    chunk = (LANES // 2 // radix, wide_lanes)
    out, marg = pl.pallas_call(
        functools.partial(window_kernel, plan),
        out_shape=(
            jax.ShapeDtypeStruct((2 * rows, LANES), f32),
            jax.ShapeDtypeStruct((own, LANES), f32),
        ),
        in_specs=[pl.BlockSpec(memory_space=pl.ANY)] * 2,
        out_specs=[pl.BlockSpec(memory_space=pl.ANY)] * 2,
        scratch_shapes=[
            pltpu.VMEM(x.shape, f32),
            pltpu.VMEM(g.shape, f32),
            pltpu.VMEM((count, rows_hi, LANES), f32),
            pltpu.VMEM((count, rows_hi, LANES), f32),
            pltpu.VMEM((2 * rows, LANES), f32),
            pltpu.VMEM((radix,) + chunk, f32),
            pltpu.VMEM((radix - 1,) + chunk, f32),
            pltpu.VMEM((own, LANES), f32),
            pltpu.SemaphoreType.DMA((2,)),
            pltpu.SemaphoreType.DMA((count - 1,)),
            pltpu.SemaphoreType.DMA((count - 1,)),
            pltpu.SemaphoreType.DMA((radix - 1,)),
            pltpu.SemaphoreType.DMA((radix - 1,)),
        ],
        compiler_params=pltpu.CompilerParams(collective_id=0, has_side_effects=True),
        name="window",
    )(x, g)
    final = jnp.swapaxes(out.reshape(rows, 2, LANES), 0, 1).reshape(1, 1, 2, amplitudes)
    return final, marg.reshape(1, -1)


def local(state, gates):
    wide_count = lax.axis_size("wide")
    narrow_count = lax.axis_size("narrow")
    amplitudes = state.shape[-1]
    found = window_plan(wide_count, narrow_count, amplitudes, gates.shape)
    if found is not None:
        return merged_local(*found, state, gates)
    flat = state.reshape(2, amplitudes)
    for layer_index in range(gates.shape[0]):
        if layer_index > 0:
            flat = rotate(flat, wide_count, narrow_count)
        flat = apply_layer(flat, gates[layer_index])
    prob = flat[0] * flat[0] + flat[1] * flat[1]
    marginal = lax.psum_scatter(prob, "narrow", scatter_dimension=0, tiled=True)
    return (flat.reshape(1, 1, 2, amplitudes), marginal.reshape(1, -1))


def solution(mesh):
    in_specs = (P(("slices", "wide"), "narrow", None, None), P())
    out_specs = (P(("slices", "wide"), "narrow", None, None), P(("slices", "wide"), "narrow"))
    return jax.shard_map(local, mesh=mesh, in_specs=in_specs, out_specs=out_specs, check_vma=False)
```

profile of v0, /device:TPU:0, one launch (start us, length us, event | category | flops | bytes accessed | tf_op | source)
XLA Modules:
  0.0 20.7 jit_solution(7200185452897214889)
XLA Ops:
  0.6 2.0 %copy.5 = f32[8,7,2,4,4]{4,3,2,1,0:T(4,128)} copy(f32[8,7,2,4,4]{0,4,3,2,1:T(4,128)} %param.3) | data formatting | bytes 14336 | tf_op args[1]
  2.6 15.9 %window.1 = (f32[256,128]{1,0:T(8,128)}, f32[32,128]{1,0:T(8,128)}) custom-call(f32[256,128]{1,0:T(8,128)} %bitcast.14, f32[112,4,4]{2,1,0:T(4,128)} %bitcast.12), custom_call_target="tpu_custom_call" | custom-call | tf_op jit(solution)/shard_map/window/pallas_call | solution.py:308
  18.5 0.0 copy-start
  18.6 1.6 %copy.9 = f32[1,1,2,16384]{3,2,1,0:T(2,128)} copy(f32[1,1,2,16384]{3,2,1,0:T(2,128)} %bitcast.13) | data formatting | bytes 262144
  20.1 0.0 copy-done
  20.1 0.6 %copy.10 = f32[1,4096]{1,0:T(1,128)} copy(f32[1,4096]{1,0:T(1,128)S(1)} %bitcast.15) | data formatting | bytes 32768
Async XLA Ops:
  18.5 1.6 %copy-start = (f32[32,128]{1,0:T(8,128)S(1)}, f32[32,128]{1,0:T(8,128)}, u32[]{:S(2)}) copy-start(f32[32,128]{1,0:T(8,128)} %get-tuple-element.5) | copy-start | bytes 49156
where the time goes:
time: 20.9 us; the launch traced here: 20.7 us
  Pallas kernels  15.9 us (76%)
  local copies, waits for them, and re-layouts  4.16 us (20%)
  between operations  0.65 us (3%)
    pallas_call x1, Pallas kernels, merged_local(): pl.pallas_call(functools.partial(window_kernel, plan), out_shape=(jax.Sha...  15.9 us
    unnamed x5, local copies, waits for them, and re-layouts  4.16 us

commit v1 on v0

--- a/solution.py
+++ b/solution.py
@@ -66,39 +66,39 @@
     )
 
 
-def small_matmul(left, right):
-    total = None
-    for index in range(right[0].shape[0]):
-        column = tuple(part[:, index : index + 1] for part in left)
-        row = tuple(part[index : index + 1, :] for part in right)
-        term = complex_mul(column, row)
-        total = term if total is None else tuple(a + b for a, b in zip(total, term))
-    return total
-
-
-def merged_gate(gate_ref, layers, pairs, shift, total_pairs, which):
+def merged_gate(planes, layers, pairs, shift, total_pairs, which):
     product = None
+    radix = planes[0][0].shape[0]
     for layer in range(layers):
         index = (which - layer * shift) % total_pairs
-        if index < pairs:
-            at = (layer * pairs + index) * 2
-            gate = (gate_ref[at], gate_ref[at + 1])
-            product = gate if product is None else small_matmul(gate, product)
-    return product
-
-
-def kron_all(members):
-    radix = members[0][0].shape[0]
+        if index >= pairs:
+            continue
+        plane = planes[index]
+        if product is not None:
+            total = None
+            for row in range(radix):
+                lane = row * layers + last
+                column = tuple(part[:, lane : lane + 1] for part in product)
+                term = complex_mul(column, tuple(part[row : row + 1, :] for part in plane))
+                total = term if total is None else (total[0] + term[0], total[1] + term[1])
+            plane = total
+        product, last = plane, layer
+    return product, last
+
+
+def kron_all(members, layers):
+    radix = members[0][0][0].shape[0]
     size = radix ** len(members)
     lane = lax.broadcasted_iota(jnp.int32, (1, size), 1)
     rows = None
-    for place, member in enumerate(reversed(members)):
+    for place, (member, last) in enumerate(reversed(members)):
         field = (lane // radix**place) % radix
         wide = []
         for part in member:
-            spread = jnp.broadcast_to(part[:, radix - 1 : radix], (radix, size))
+            columns = [part[:, index * layers + last : index * layers + last + 1] for index in range(radix)]
+            spread = jnp.broadcast_to(columns[-1], (radix, size))
             for index in range(radix - 1):
-                spread = jnp.where(field == index, part[:, index : index + 1], spread)
+                spread = jnp.where(field == index, columns[index], spread)
             wide.append(spread)
         if rows is None:
             rows = tuple(wide)
@@ -116,9 +116,9 @@
     return high, (value - high.astype(jnp.float32)).astype(jnp.bfloat16)
 
 
-def dot_t(left, right):
+def dot(left, right, contract):
     def one(a, b):
-        return lax.dot_general(a, b, (((1,), (1,)), ((), ())), preferred_element_type=jnp.float32)
+        return lax.dot_general(a, b, (((1,), (contract,)), ((), ())), preferred_element_type=jnp.float32)
 
     return one(left[0], right[0]) + (one(left[0], right[1]) + one(left[1], right[0]))
 
@@ -143,7 +143,19 @@
     copy_x.start()
     copy_g.wait()
 
-    gate_of = functools.partial(merged_gate, g, layers, pairs, shift, total_pairs)
+    planes = []
+    for index in range(pairs):
+        plane = []
+        for c in range(2):
+            total = None
+            for row in range(radix):
+                tile = g[(index * 2 + c) * radix + row]
+                tile = jnp.concatenate([tile, jnp.zeros((radix, LANES - layers), jnp.float32)], axis=1)
+                tile = pltpu.roll(tile, row * layers, 1) if row else tile
+                total = tile if total is None else total + tile
+            plane.append(total)
+        planes.append(tuple(plane))
+    gate_of = functools.partial(merged_gate, planes, layers, pairs, shift, total_pairs)
     low_gate = gate_of(start)
     high_gate = gate_of(start + 1)
 
@@ -154,8 +166,9 @@
     shape = (rows_hi, LANES)
 
     def entry(gate, row, column):
+        lane_at = row * layers + gate[1]
         return tuple(
-            jnp.broadcast_to(part_[row : row + 1, column : column + 1], shape) for part_ in gate
+            jnp.broadcast_to(item[column : column + 1, lane_at : lane_at + 1], shape) for item in gate[0]
         )
 
     def both(gate, one, other):
@@ -209,27 +222,25 @@
         copies.append(copy)
     recv[me] = send[me]
 
-    low = kron_all([gate_of(which) for which in range(start - 1, -1, -1)])
-    lane_form = split(
-        jnp.concatenate(
-            [
-                jnp.concatenate([low[0], -low[1]], axis=1),
-                jnp.concatenate([low[1], low[0]], axis=1),
-            ],
-            axis=0,
-        )
-    )
-    row_real, row_imag = kron_all([gate_of(which) for which in range(total_pairs - 1, start + 1, -1)])
-    row_real = split(row_real)
-    row_imag = split(row_imag)
+    low = kron_all([gate_of(which) for which in range(start - 1, -1, -1)], layers)
+    lane_form = jnp.concatenate(
+        [
+            jnp.concatenate([low[0], low[1]], axis=1),
+            jnp.concatenate([-low[1], low[0]], axis=1),
+        ],
+        axis=0,
+    )
+    lane_form = split(lane_form.T)
+    row_members = [gate_of(which) for which in range(total_pairs - 1, start + 1, -1)]
+    row_real, row_imag = (split(item) for item in kron_all(row_members, layers))
 
     for copy in copies:
         copy.wait_recv()
     count = radix * radix
     size = count * rows_hi
-    turned = split(dot_t(lane_form, split(recv[...].reshape(size, LANES))))
-    with_real = dot_t(turned, row_real)
-    with_imag = dot_t(turned, row_imag)
+    turned = split(dot(lane_form, split(recv[...].reshape(size, LANES)), 1))
+    with_real = dot(turned, row_real, 0)
+    with_imag = dot(turned, row_imag, 0)
     real = with_real[:half] - with_imag[half:]
     imag = with_real[half:] + with_imag[:half]
     density = real * real + imag * imag
@@ -283,7 +294,7 @@
         return None
     offset = ((layers - 1) * high_bits) % total_bits
     start = offset // 2 - high_bits // 2
-    if start < 1 or offset // 2 >= pairs or 2 * radix**start != LANES:
+    if layers * radix > LANES or start < 1 or offset // 2 >= pairs or 2 * radix**start != LANES:
         return None
     rows_hi = radix ** (pairs - offset // 2)
     if rows_hi % 8:
@@ -301,7 +312,7 @@
     count = radix * radix
     own = amplitudes // radix // LANES
     x = jnp.swapaxes(state.reshape(2, rows, LANES), 0, 1).reshape(2 * rows, LANES)
-    g = gates.reshape(-1, radix, radix)
+    g = jnp.transpose(gates, (1, 2, 3, 4, 0)).reshape(-1, radix, gates.shape[0])
     f32 = jnp.float32
     wide_lanes = count * rows_hi
     chunk = (LANES // 2 // radix, wide_lanes)
@@ -311,7 +322,7 @@
             jax.ShapeDtypeStruct((2 * rows, LANES), f32),
             jax.ShapeDtypeStruct((own, LANES), f32),
         ),
-        in_specs=[pl.BlockSpec(memory_space=pl.ANY)] * 2,
+        in_specs=[pl.BlockSpec(memory_space=pltpu.HBM)] * 2,
         out_specs=[pl.BlockSpec(memory_space=pl.ANY)] * 2,
         scratch_shapes=[
             pltpu.VMEM(x.shape, f32),
@@ -328,7 +339,9 @@
             pltpu.SemaphoreType.DMA((radix - 1,)),
             pltpu.SemaphoreType.DMA((radix - 1,)),
         ],
-        compiler_params=pltpu.CompilerParams(collective_id=0, has_side_effects=True),
+        compiler_params=pltpu.CompilerParams(
+            collective_id=0, has_side_effects=True, vmem_limit_bytes=8 * 2**20
+        ),
         name="window",
     )(x, g)
     final = jnp.swapaxes(out.reshape(rows, 2, LANES), 0, 1).reshape(1, 1, 2, amplitudes)

time: 20.9 us -> 20.4 us (0.976)
  local copies, waits for them, and re-layouts: 4.16 us -> 3.06 us
  Pallas kernels: 15.9 us -> 16.6 us
    unnamed x5 -> x6, local copies, waits for them, and re-layouts: 4.16 us -> 3.06 us
    pallas_call x1, Pallas kernels: 15.9 us -> 16.6 us  [merged_local(): pl.pallas_call(functools.partial(window_kernel, plan), out_shape=(jax.Sha...]
where the time goes in v1:
time: 20.4 us; the launch traced here: 20.3 us
  Pallas kernels  16.6 us (81%)
  local copies, waits for them, and re-layouts  3.06 us (15%)
  between operations  0.65 us (3%)
    pallas_call x1, Pallas kernels, merged_local(): pl.pallas_call(functools.partial(window_kernel, plan), out_shape=(jax.Sha...  16.6 us
    unnamed x6, local copies, waits for them, and re-layouts  3.06 us

profile of v1, /device:TPU:0, one launch (start us, length us, event | category | flops | bytes accessed | tf_op | source)
XLA Modules:
  0.0 20.3 jit_solution(10216032432904276686)
XLA Ops:
  0.6 0.0 copy-start
  0.6 0.9 %copy-done = f32[1,1,2,16384]{3,2,1,0:T(2,128)S(1)} copy-done((f32[1,1,2,16384]{3,2,1,0:T(2,128)S(1)}, f32[1,1,2,16384]{3,2,1,0:T(2,128)}, u32[]{:S(2)}) %copy-start) | copy-done | bytes 131096
  1.5 0.0 copy-start.1
  1.5 0.9 %copy-done.1 = f32[8,7,2,4,4]{0,4,3,2,1:T(4,128)S(1)} copy-done((f32[8,7,2,4,4]{0,4,3,2,1:T(4,128)S(1)}, f32[8,7,2,4,4]{0,4,3,2,1:T(4,128)}, u32[]{:S(2)}) %copy-start.1) | copy-done | bytes 7192
  2.4 16.6 %window.1 = (f32[256,128]{1,0:T(8,128)S(1)}, f32[32,128]{1,0:T(8,128)S(1)}) custom-call(f32[256,128]{1,0:T(8,128)S(1)} %bitcast.15, f32[56,4,8]{2,1,0:T(4,128)S(1)} %bitcast.16), custom_call_target="tpu_custom_call" | custom-call | tf_op jit(solution)/shard_map/window/pallas_call | solution.py:319
  19.0 0.7 %copy.8 = f32[1,1,2,16384]{3,2,1,0:T(2,128)} copy(f32[1,1,2,16384]{3,2,1,0:T(2,128)S(1)} %bitcast.14) | data formatting | bytes 262144
  19.7 0.6 %copy.9 = f32[1,4096]{1,0:T(1,128)} copy(f32[1,4096]{1,0:T(1,128)S(1)} %bitcast.17) | data formatting | bytes 32768
Async XLA Ops:
  0.6 0.9 %copy-start = (f32[1,1,2,16384]{3,2,1,0:T(2,128)S(1)}, f32[1,1,2,16384]{3,2,1,0:T(2,128)}, u32[]{:S(2)}) copy-start(f32[1,1,2,16384]{3,2,1,0:T(2,128)} %param.2) | copy-start | bytes 393220
  1.5 0.9 %copy-start.1 = (f32[8,7,2,4,4]{0,4,3,2,1:T(4,128)S(1)}, f32[8,7,2,4,4]{0,4,3,2,1:T(4,128)}, u32[]{:S(2)}) copy-start(f32[8,7,2,4,4]{0,4,3,2,1:T(4,128)} %param.3) | copy-start | bytes 21508

commit v2 on v1

--- a/solution.py
+++ b/solution.py
@@ -123,8 +123,8 @@
     return one(left[0], right[0]) + (one(left[0], right[1]) + one(left[1], right[0]))
 
 
-def window_kernel(plan, x_hbm, g_hbm, out_hbm, marg_hbm, x, g, send, recv, fin, prob, part, marg,
-                  local_sem, send_sem, recv_sem, psend_sem, precv_sem):
+def exchange_kernel(plan, x_hbm, g_hbm, recv, lane_hi, lane_lo, row_hi, row_lo, x, g, send,
+                    local_sem, send_sem, recv_sem):
     layers, pairs, shift, total_pairs, start, radix = plan
     w = lax.axis_index("wide")
     n = lax.axis_index("narrow")
@@ -156,14 +156,17 @@
             plane.append(total)
         planes.append(tuple(plane))
     gate_of = functools.partial(merged_gate, planes, layers, pairs, shift, total_pairs)
+    split_gate = gate_of(start - 1)
     low_gate = gate_of(start)
     high_gate = gate_of(start + 1)
 
     half = LANES // 2
-    rows_hi = send.shape[1]
-    lane = lax.broadcasted_iota(jnp.int32, (rows_hi, LANES), 1)
+    group = half // radix
+    rows_hi = send.shape[1] // 2
+    shape = (rows_hi, LANES)
+    lane = lax.broadcasted_iota(jnp.int32, shape, 1)
     first = lane < half
-    shape = (rows_hi, LANES)
+    field = (lane // group) % radix
 
     def entry(gate, row, column):
         lane_at = row * layers + gate[1]
@@ -176,6 +179,16 @@
 
     def add(total, term):
         return term if total is None else (total[0] + term[0], total[1] + term[1])
+
+    def roll(value, amount):
+        amount %= LANES
+        return pltpu.roll(value, amount, 1) if amount else value
+
+    steps = {}
+    for row in range(radix):
+        for column in range(radix):
+            item = tuple(jnp.where(field == row, part, 0.0) for part in entry(split_gate, row, column))
+            steps[column - row] = add(steps.get(column - row), item)
 
     copy_x.wait()
     same = [[both(low_gate, (2 * o, 2 * i), (2 * o + 1, 2 * i + 1)) for i in range(2)] for o in range(2)]
@@ -186,7 +199,7 @@
         held = []
         for i in range(2):
             held.append(tuple(x[pl.ds(high * 4 + i * 2 + c, rows_hi, stride=stride), :] for c in range(2)))
-        turned = [tuple(pltpu.roll(v, half, 1) for v in pair) for pair in held]
+        turned = [tuple(roll(v, half) for v in pair) for pair in held]
         result = []
         for o in range(2):
             total = None
@@ -197,13 +210,26 @@
         stage.append(result)
     for out_high in range(radix):
         coefs = [entry(high_gate, out_high, high) for high in range(radix)]
+        ready = []
         for o in range(2):
             total = None
             for high in range(radix):
                 total = add(total, complex_mul(coefs[high], stage[high][o]))
-            rolled = tuple(pltpu.roll(v, half, 1) for v in total)
-            send[out_high * radix + 2 * o] = jnp.where(first, total[0], rolled[1])
-            send[out_high * radix + 2 * o + 1] = jnp.where(first, rolled[0], total[1])
+            mixed = None
+            for step, coef in steps.items():
+                mixed = add(mixed, complex_mul(coef, tuple(roll(v, -group * step) for v in total)))
+            ready.append(mixed)
+            rolled = tuple(roll(v, half) for v in mixed)
+            at = out_high * radix + 2 * o
+            send[at, :rows_hi] = jnp.where(first, mixed[0], rolled[1])
+            send[at + 1, :rows_hi] = jnp.where(first, rolled[0], mixed[1])
+        for take in range(radix):
+            block = None
+            for o in range(2):
+                for c in range(2):
+                    piece = roll(ready[o][c], (2 * o + c - take) * group)
+                    block = piece if block is None else jnp.where(field == 2 * o + c, piece, block)
+            send[out_high * radix + take, rows_hi:] = block
 
     pl.semaphore_wait(barrier, len(offsets))
     me = w * radix + n
@@ -222,63 +248,65 @@
         copies.append(copy)
     recv[me] = send[me]
 
-    low = kron_all([gate_of(which) for which in range(start - 1, -1, -1)], layers)
-    lane_form = jnp.concatenate(
-        [
-            jnp.concatenate([low[0], low[1]], axis=1),
-            jnp.concatenate([-low[1], low[0]], axis=1),
-        ],
+    low = kron_all([gate_of(which) for which in range(start - 2, -1, -1)], layers)
+    block = jnp.concatenate(
+        [jnp.concatenate([low[0], low[1]], axis=1), jnp.concatenate([-low[1], low[0]], axis=1)], axis=0
+    )
+    block = jnp.concatenate([jnp.concatenate([block] * radix, axis=0)] * radix, axis=1)
+    down = lax.broadcasted_iota(jnp.int32, (LANES, LANES), 0)
+    across = lax.broadcasted_iota(jnp.int32, (LANES, LANES), 1)
+    grouped = jnp.where(down // (2 * group) == across // (2 * group), block, 0.0).T
+    parts = [jnp.concatenate([jnp.concatenate([item] * radix, axis=0)] * radix, axis=1) for item in low]
+    keep = (down[:half, :half] // group) == (across[:half, :half] // group)
+    parts = [jnp.where(keep, item, 0.0) for item in parts]
+    plain = jnp.concatenate(
+        [jnp.concatenate([parts[0], parts[1]], axis=1), jnp.concatenate([-parts[1], parts[0]], axis=1)],
         axis=0,
-    )
-    lane_form = split(lane_form.T)
+    ).T
+    for index, item in enumerate((plain, grouped)):
+        lane_hi[index], lane_lo[index] = split(item)
     row_members = [gate_of(which) for which in range(total_pairs - 1, start + 1, -1)]
-    row_real, row_imag = (split(item) for item in kron_all(row_members, layers))
+    for index, item in enumerate(kron_all(row_members, layers)):
+        row_hi[index], row_lo[index] = split(item)
 
     for copy in copies:
-        copy.wait_recv()
-    count = radix * radix
-    size = count * rows_hi
-    turned = split(dot(lane_form, split(recv[...].reshape(size, LANES)), 1))
-    with_real = dot(turned, row_real, 0)
-    with_imag = dot(turned, row_imag, 0)
+        copy.wait()
+
+
+def finish_kernel(radix, recv, lane_hi, lane_lo, row_hi, row_lo, out_hbm, marg_hbm, fin, marg, sems):
+    rows_hi = recv.shape[1] // 2
+    size = recv.shape[0] * rows_hi
+    half = LANES // 2
+    group = half // radix
+    blocks = size // LANES
+    rows = (row_hi[0], row_lo[0]), (row_hi[1], row_lo[1])
+
+    def apply(which):
+        held = split(recv[:, which * rows_hi : (which + 1) * rows_hi].reshape(size, LANES))
+        turned = split(dot((lane_hi[which], lane_lo[which]), held, 1))
+        return dot(turned, rows[0], 0), dot(turned, rows[1], 0)
+
+    with_real, with_imag = apply(0)
     real = with_real[:half] - with_imag[half:]
     imag = with_real[half:] + with_imag[:half]
-    density = real * real + imag * imag
-    own_rows = half // radix
-    for index in range(radix):
-        prob[index] = density[index * own_rows : (index + 1) * own_rows]
-    blocks = size // LANES
     for block in range(blocks):
         columns = slice(block * LANES, (block + 1) * LANES)
         fin[pl.ds(block * 2, half, stride=2 * blocks), :] = real[:, columns]
         fin[pl.ds(block * 2 + 1, half, stride=2 * blocks), :] = imag[:, columns]
-    sums = []
-    for dn in range(1, radix):
-        pn = lax.rem(n + dn, radix)
-        copy = pltpu.make_async_remote_copy(
-            src_ref=prob.at[pn],
-            dst_ref=part.at[dn - 1],
-            send_sem=psend_sem.at[dn - 1],
-            recv_sem=precv_sem.at[dn - 1],
-            device_id={"wide": w, "narrow": pn},
-            device_id_type=MESH,
-        )
-        copy.start()
-        sums.append(copy)
-    out_copy = pltpu.make_async_copy(fin, out_hbm, local_sem.at[0])
+    out_copy = pltpu.make_async_copy(fin, out_hbm, sems.at[0])
     out_copy.start()
-    for copy in copies:
-        copy.wait_send()
-    total = prob[n]
-    for index, copy in enumerate(sums):
-        copy.wait_recv()
-        total = total + part[index]
+    with_real, with_imag = apply(1)
+    total = None
+    for index in range(radix):
+        at = 2 * group * index
+        real = with_real[at : at + group] - with_imag[at + group : at + 2 * group]
+        imag = with_real[at + group : at + 2 * group] + with_imag[at : at + group]
+        term = real * real + imag * imag
+        total = term if total is None else total + term
     for block in range(blocks):
-        marg[pl.ds(block, own_rows, stride=blocks), :] = total[:, block * LANES : (block + 1) * LANES]
-    marg_copy = pltpu.make_async_copy(marg, marg_hbm, local_sem.at[1])
+        marg[pl.ds(block, group, stride=blocks), :] = total[:, block * LANES : (block + 1) * LANES]
+    marg_copy = pltpu.make_async_copy(marg, marg_hbm, sems.at[1])
     marg_copy.start()
-    for copy in sums:
-        copy.wait_send()
     out_copy.wait()
     marg_copy.wait()
 
@@ -294,7 +322,7 @@
         return None
     offset = ((layers - 1) * high_bits) % total_bits
     start = offset // 2 - high_bits // 2
-    if layers * radix > LANES or start < 1 or offset // 2 >= pairs or 2 * radix**start != LANES:
+    if layers * radix > LANES or start < 2 or offset // 2 >= pairs or 2 * radix**start != LANES:
         return None
     rows_hi = radix ** (pairs - offset // 2)
     if rows_hi % 8:
@@ -313,37 +341,49 @@
     own = amplitudes // radix // LANES
     x = jnp.swapaxes(state.reshape(2, rows, LANES), 0, 1).reshape(2 * rows, LANES)
     g = jnp.transpose(gates, (1, 2, 3, 4, 0)).reshape(-1, radix, gates.shape[0])
-    f32 = jnp.float32
-    wide_lanes = count * rows_hi
-    chunk = (LANES // 2 // radix, wide_lanes)
-    out, marg = pl.pallas_call(
-        functools.partial(window_kernel, plan),
-        out_shape=(
-            jax.ShapeDtypeStruct((2 * rows, LANES), f32),
-            jax.ShapeDtypeStruct((own, LANES), f32),
-        ),
+    f32, bf16 = jnp.float32, jnp.bfloat16
+    size = count * rows_hi
+    shared = (
+        pltpu.VMEM((count, 2 * rows_hi, LANES), f32),
+        pltpu.VMEM((2, LANES, LANES), bf16),
+        pltpu.VMEM((2, LANES, LANES), bf16),
+        pltpu.VMEM((2, size, size), bf16),
+        pltpu.VMEM((2, size, size), bf16),
+    )
+    held = pl.pallas_call(
+        functools.partial(exchange_kernel, plan),
+        out_shape=shared,
         in_specs=[pl.BlockSpec(memory_space=pltpu.HBM)] * 2,
-        out_specs=[pl.BlockSpec(memory_space=pl.ANY)] * 2,
+        out_specs=[pl.BlockSpec(memory_space=pltpu.VMEM)] * len(shared),
         scratch_shapes=[
             pltpu.VMEM(x.shape, f32),
             pltpu.VMEM(g.shape, f32),
-            pltpu.VMEM((count, rows_hi, LANES), f32),
-            pltpu.VMEM((count, rows_hi, LANES), f32),
-            pltpu.VMEM((2 * rows, LANES), f32),
-            pltpu.VMEM((radix,) + chunk, f32),
-            pltpu.VMEM((radix - 1,) + chunk, f32),
-            pltpu.VMEM((own, LANES), f32),
+            pltpu.VMEM((count, 2 * rows_hi, LANES), f32),
             pltpu.SemaphoreType.DMA((2,)),
             pltpu.SemaphoreType.DMA((count - 1,)),
             pltpu.SemaphoreType.DMA((count - 1,)),
-            pltpu.SemaphoreType.DMA((radix - 1,)),
-            pltpu.SemaphoreType.DMA((radix - 1,)),
         ],
         compiler_params=pltpu.CompilerParams(
             collective_id=0, has_side_effects=True, vmem_limit_bytes=8 * 2**20
         ),
-        name="window",
-    )(x, g)
+        name="exchange",
+    )(
+        pltpu.with_memory_space_constraint(x, pltpu.HBM),
+        pltpu.with_memory_space_constraint(g, pltpu.HBM),
+    )
+    out, marg = pl.pallas_call(
+        functools.partial(finish_kernel, radix),
+        out_shape=(pltpu.HBM((2 * rows, LANES), f32), pltpu.HBM((own, LANES), f32)),
+        in_specs=[pl.BlockSpec(memory_space=pltpu.VMEM)] * len(shared),
+        out_specs=[pl.BlockSpec(memory_space=pltpu.HBM)] * 2,
+        scratch_shapes=[
+            pltpu.VMEM((2 * rows, LANES), f32),
+            pltpu.VMEM((own, LANES), f32),
+            pltpu.SemaphoreType.DMA((2,)),
+        ],
+        compiler_params=pltpu.CompilerParams(vmem_limit_bytes=8 * 2**20),
+        name="finish",
+    )(*held)
     final = jnp.swapaxes(out.reshape(rows, 2, LANES), 0, 1).reshape(1, 1, 2, amplitudes)
     return final, marg.reshape(1, -1)
 

time: 20.4 us -> 17.3 us (0.85)
  local copies, waits for them, and re-layouts: 3.06 us -> 0 us
    unnamed x6 -> x0, local copies, waits for them, and re-layouts: 3.06 us -> none
    pallas_call x1 -> x2, Pallas kernels: 16.6 us -> 16.5 us  [the longest x1 15.2 us: merged_local(): pl.pallas_call(functools.partial(exchange_kernel, plan), out_shape=shared...]
where the time goes in v2:
time: 17.3 us; the launch traced here: 17.1 us
  Pallas kernels  16.5 us (95%)
  between operations  0.64 us (4%)
    pallas_call x1, Pallas kernels, merged_local(): pl.pallas_call(functools.partial(exchange_kernel, plan), out_shape=shared...  15.2 us
    pallas_call x1, Pallas kernels, merged_local(): pl.pallas_call(functools.partial(finish_kernel, radix), out_shape=(pltpu....  1.26 us

profile of v2, /device:TPU:0, one launch (start us, length us, event | category | flops | bytes accessed | tf_op | source)
XLA Modules:
  0.0 17.1 jit_solution(9136106127415897431)
XLA Ops:
  0.6 15.2 %exchange.1 = (f32[16,32,128]{2,1,0:T(8,128)S(1)}, bf16[2,128,128]{2,1,0:T(8,128)(2,1)S(1)}, bf16[2,128,128]{2,1,0:T(8,128)(2,1)S(1)}, bf16[2,256,256]{2,1,0:T(8,128)(2,1)S(1)}, bf16[2,256,256]{2,1,0:T(8,128)(2,1)S(1)}) custom-call(f32[256,128]{1,0:T(8,128)} %bitcast.14, f32[56,4,8]{2,1,0:T(4,128)} %bitcast.15), custom_call_target="tpu_custom_call" | custom-call | tf_op jit(solution)/shard_map/exchange/pallas_call | solution.py:353
  15.9 1.3 %finish.1 = (f32[256,128]{1,0:T(8,128)}, f32[32,128]{1,0:T(8,128)}) custom-call(f32[16,32,128]{2,1,0:T(8,128)S(1)} %get-tuple-element.9.recv, bf16[2,128,128]{2,1,0:T(8,128)(2,1)S(1)} %get-tuple-element.10.lane_hi, bf16[2,128,128]{2,1,0:T(8,128)(2,1)S(1)} %get-tuple-element.11.lane_lo, bf16[2,256,256]{2,1,0:T(8,128)(2,1)S(1)} %get-tuple-element.12.row_hi, ...), custom_call_target="tpu_custom_call" | custom-call | tf_op jit(solution)/shard_map/finish/pallas_call | solution.py:374

commit v3 on v2

--- a/solution.py
+++ b/solution.py
@@ -66,24 +66,35 @@
     )
 
 
-def merged_gate(planes, layers, pairs, shift, total_pairs, which):
-    product = None
-    radix = planes[0][0].shape[0]
+def merged_gates(planes, plan, which):
+    layers, pairs, shift, total_pairs, _, radix = plan
+    lane = lax.broadcasted_iota(jnp.int32, planes[0][0].shape, 1)
+    down = lax.broadcasted_iota(jnp.int32, planes[0][0].shape, 0)
+    unit = jnp.where(lane // layers == down, 1.0, 0.0)
+    unit = (unit, jnp.zeros_like(unit))
+    items = []
     for layer in range(layers):
-        index = (which - layer * shift) % total_pairs
-        if index >= pairs:
-            continue
-        plane = planes[index]
-        if product is not None:
+        places = [(pair - layer * shift) % total_pairs for pair in which]
+        chosen = [planes[place] if place < pairs else unit for place in places]
+        items.append((tuple(jnp.stack([gate[c] for gate in chosen]) for c in range(2)), layer))
+    while len(items) > 1:
+        joined = []
+        for at in range(0, len(items) - 1, 2):
+            (early, last), (late, newest) = items[at], items[at + 1]
             total = None
             for row in range(radix):
-                lane = row * layers + last
-                column = tuple(part[:, lane : lane + 1] for part in product)
-                term = complex_mul(column, tuple(part[row : row + 1, :] for part in plane))
+                lane_at = row * layers + last
+                term = complex_mul(
+                    tuple(part[:, :, lane_at : lane_at + 1] for part in early),
+                    tuple(part[:, row : row + 1, :] for part in late),
+                )
                 total = term if total is None else (total[0] + term[0], total[1] + term[1])
-            plane = total
-        product, last = plane, layer
-    return product, last
+            joined.append((total, newest))
+        if len(items) % 2:
+            joined.append(items[-1])
+        items = joined
+    parts, last = items[0]
+    return [(tuple(part[index] for part in parts), last) for index in range(len(which))]
 
 
 def kron_all(members, layers):
@@ -155,10 +166,7 @@
                 total = tile if total is None else total + tile
             plane.append(total)
         planes.append(tuple(plane))
-    gate_of = functools.partial(merged_gate, planes, layers, pairs, shift, total_pairs)
-    split_gate = gate_of(start - 1)
-    low_gate = gate_of(start)
-    high_gate = gate_of(start + 1)
+    split_gate, low_gate, high_gate = merged_gates(planes, plan, range(start - 1, start + 2))
 
     half = LANES // 2
     group = half // radix
@@ -233,14 +241,17 @@
 
     pl.semaphore_wait(barrier, len(offsets))
     me = w * radix + n
+    count = radix * radix
+    seat = n * radix + w
     copies = []
-    for at, (dw, dn) in enumerate(offsets):
-        pw, pn = partner(dw, dn)
+    for at in range(count - 1):
+        other = at + (at + count - seat) // count
+        pw, pn = other % radix, other // radix
         copy = pltpu.make_async_remote_copy(
             src_ref=send.at[pw * radix + pn],
             dst_ref=recv.at[me],
-            send_sem=send_sem.at[at],
-            recv_sem=recv_sem.at[at],
+            send_sem=send_sem.at[other],
+            recv_sem=recv_sem.at[seat],
             device_id={"wide": pw, "narrow": pn},
             device_id_type=MESH,
         )
@@ -248,7 +259,9 @@
         copies.append(copy)
     recv[me] = send[me]
 
-    low = kron_all([gate_of(which) for which in range(start - 2, -1, -1)], layers)
+    rest = list(range(start - 1)) + list(range(start + 2, total_pairs))
+    rest = dict(zip(rest, merged_gates(planes, plan, rest)))
+    low = kron_all([rest[pair] for pair in range(start - 2, -1, -1)], layers)
     block = jnp.concatenate(
         [jnp.concatenate([low[0], low[1]], axis=1), jnp.concatenate([-low[1], low[0]], axis=1)], axis=0
     )
@@ -265,12 +278,23 @@
     ).T
     for index, item in enumerate((plain, grouped)):
         lane_hi[index], lane_lo[index] = split(item)
-    row_members = [gate_of(which) for which in range(total_pairs - 1, start + 1, -1)]
+    row_members = [rest[pair] for pair in range(total_pairs - 1, start + 1, -1)]
     for index, item in enumerate(kron_all(row_members, layers)):
         row_hi[index], row_lo[index] = split(item)
 
     for copy in copies:
-        copy.wait()
+        copy.wait_send()
+    for at in range(count - 1):
+        other = at + (at + count - seat) // count
+        pw, pn = other % radix, other // radix
+        pltpu.make_async_remote_copy(
+            src_ref=send.at[me],
+            dst_ref=recv.at[pw * radix + pn],
+            send_sem=send_sem.at[other],
+            recv_sem=recv_sem.at[other],
+            device_id={"wide": pw, "narrow": pn},
+            device_id_type=MESH,
+        ).wait_recv()
 
 
 def finish_kernel(radix, recv, lane_hi, lane_lo, row_hi, row_lo, out_hbm, marg_hbm, fin, marg, sems):
@@ -360,8 +384,8 @@
             pltpu.VMEM(g.shape, f32),
             pltpu.VMEM((count, 2 * rows_hi, LANES), f32),
             pltpu.SemaphoreType.DMA((2,)),
-            pltpu.SemaphoreType.DMA((count - 1,)),
-            pltpu.SemaphoreType.DMA((count - 1,)),
+            pltpu.SemaphoreType.DMA((count,)),
+            pltpu.SemaphoreType.DMA((count,)),
         ],
         compiler_params=pltpu.CompilerParams(
             collective_id=0, has_side_effects=True, vmem_limit_bytes=8 * 2**20

time: 17.3 us -> 14.8 us (0.86)
  Pallas kernels: 16.5 us -> 14 us
    pallas_call x1, Pallas kernels: 15.2 us -> 12.7 us  [merged_local(): pl.pallas_call(functools.partial(exchange_kernel, plan), out_shape=shared...]
where the time goes in v3:
time: 14.8 us; the launch traced here: 14.6 us
  Pallas kernels  14 us (95%)
  between operations  0.64 us (4%)
    pallas_call x1, Pallas kernels, merged_local(): pl.pallas_call(functools.partial(exchange_kernel, plan), out_shape=shared...  12.7 us
    pallas_call x1, Pallas kernels, merged_local(): pl.pallas_call(functools.partial(finish_kernel, radix), out_shape=(pltpu....  1.26 us

profile of v3, /device:TPU:0, one launch (start us, length us, event | category | flops | bytes accessed | tf_op | source)
XLA Modules:
  0.0 14.6 jit_solution(12693160918193729614)
XLA Ops:
  0.6 12.7 %exchange.1 = (f32[16,32,128]{2,1,0:T(8,128)S(1)}, bf16[2,128,128]{2,1,0:T(8,128)(2,1)S(1)}, bf16[2,128,128]{2,1,0:T(8,128)(2,1)S(1)}, bf16[2,256,256]{2,1,0:T(8,128)(2,1)S(1)}, bf16[2,256,256]{2,1,0:T(8,128)(2,1)S(1)}) custom-call(f32[256,128]{1,0:T(8,128)} %bitcast.14, f32[56,4,8]{2,1,0:T(4,128)} %bitcast.15), custom_call_target="tpu_custom_call" | custom-call | tf_op jit(solution)/shard_map/exchange/pallas_call | solution.py:377
  13.4 1.3 %finish.1 = (f32[256,128]{1,0:T(8,128)}, f32[32,128]{1,0:T(8,128)}) custom-call(f32[16,32,128]{2,1,0:T(8,128)S(1)} %get-tuple-element.9.recv, bf16[2,128,128]{2,1,0:T(8,128)(2,1)S(1)} %get-tuple-element.10.lane_hi, bf16[2,128,128]{2,1,0:T(8,128)(2,1)S(1)} %get-tuple-element.11.lane_lo, bf16[2,256,256]{2,1,0:T(8,128)(2,1)S(1)} %get-tuple-element.12.row_hi, ...), custom_call_target="tpu_custom_call" | custom-call | tf_op jit(solution)/shard_map/finish/pallas_call | solution.py:398

commit v4 on v3

--- a/solution.py
+++ b/solution.py
@@ -170,11 +170,13 @@
 
     half = LANES // 2
     group = half // radix
-    rows_hi = send.shape[1] // 2
+    rows_hi = send.shape[1] * radix // (2 * radix - 1)
+    tail = rows_hi // radix
     shape = (rows_hi, LANES)
     lane = lax.broadcasted_iota(jnp.int32, shape, 1)
     first = lane < half
     field = (lane // group) % radix
+    outer = lane // (2 * group)
 
     def entry(gate, row, column):
         lane_at = row * layers + gate[1]
@@ -237,7 +239,15 @@
                 for c in range(2):
                     piece = roll(ready[o][c], (2 * o + c - take) * group)
                     block = piece if block is None else jnp.where(field == 2 * o + c, piece, block)
-            send[out_high * radix + take, rows_hi:] = block
+            spare = (take % 2) * 2 + take // 2
+            if spare != radix - 1:
+                block = jnp.where(outer == spare, roll(block, 2 * group * (spare + 1)), block)
+            moved = [roll(block[rows_hi - tail :], -2 * group * (k + 1)) for k in range(radix - 1)]
+            send[out_high * radix + take, rows_hi:] = jnp.where(
+                outer[: rows_hi - tail] == radix - 1,
+                jnp.concatenate(moved, axis=0),
+                block[: rows_hi - tail],
+            )
 
     pl.semaphore_wait(barrier, len(offsets))
     me = w * radix + n
@@ -297,20 +307,22 @@
         ).wait_recv()
 
 
-def finish_kernel(radix, recv, lane_hi, lane_lo, row_hi, row_lo, out_hbm, marg_hbm, fin, marg, sems):
-    rows_hi = recv.shape[1] // 2
+def finish_kernel(radix, recv, lane_hi, lane_lo, row_hi, row_lo, out_hbm, marg_hbm, fin, prob, marg, sems):
+    rows_hi = recv.shape[1] * radix // (2 * radix - 1)
+    tail = rows_hi // radix
     size = recv.shape[0] * rows_hi
     half = LANES // 2
     group = half // radix
     blocks = size // LANES
     rows = (row_hi[0], row_lo[0]), (row_hi[1], row_lo[1])
 
-    def apply(which):
-        held = split(recv[:, which * rows_hi : (which + 1) * rows_hi].reshape(size, LANES))
-        turned = split(dot((lane_hi[which], lane_lo[which]), held, 1))
+    def apply(which, value, keep):
+        held = split(value.reshape(size, LANES))
+        turned = dot((lane_hi[which], lane_lo[which]), held, 1)
+        turned = split(turned[:keep])
         return dot(turned, rows[0], 0), dot(turned, rows[1], 0)
 
-    with_real, with_imag = apply(0)
+    with_real, with_imag = apply(0, recv[:, :rows_hi], LANES)
     real = with_real[:half] - with_imag[half:]
     imag = with_real[half:] + with_imag[:half]
     for block in range(blocks):
@@ -319,14 +331,25 @@
         fin[pl.ds(block * 2 + 1, half, stride=2 * blocks), :] = imag[:, columns]
     out_copy = pltpu.make_async_copy(fin, out_hbm, sems.at[0])
     out_copy.start()
-    with_real, with_imag = apply(1)
-    total = None
+    density = real * real + imag * imag
     for index in range(radix):
+        prob[index] = density[index * group : (index + 1) * group]
+    packed = recv[:, rows_hi:]
+    outer = lax.broadcasted_iota(jnp.int32, (1, tail, LANES), 2) // (2 * group)
+    last = None
+    for index in range(radix - 1):
+        piece = packed[:, index * tail : (index + 1) * tail]
+        piece = pltpu.roll(piece, 2 * group * (index + 1), 2)
+        last = piece if last is None else jnp.where(outer == index, piece, last)
+    wide = jnp.concatenate([packed, last], axis=1)
+    with_real, with_imag = apply(1, wide, LANES - 2 * group)
+    total = prob[lax.axis_index("narrow")]
+    for index in range(radix - 1):
         at = 2 * group * index
         real = with_real[at : at + group] - with_imag[at + group : at + 2 * group]
         imag = with_real[at + group : at + 2 * group] + with_imag[at : at + group]
         term = real * real + imag * imag
-        total = term if total is None else total + term
+        total = total + term
     for block in range(blocks):
         marg[pl.ds(block, group, stride=blocks), :] = total[:, block * LANES : (block + 1) * LANES]
     marg_copy = pltpu.make_async_copy(marg, marg_hbm, sems.at[1])
@@ -367,8 +390,9 @@
     g = jnp.transpose(gates, (1, 2, 3, 4, 0)).reshape(-1, radix, gates.shape[0])
     f32, bf16 = jnp.float32, jnp.bfloat16
     size = count * rows_hi
+    message = 2 * rows_hi - rows_hi // radix
     shared = (
-        pltpu.VMEM((count, 2 * rows_hi, LANES), f32),
+        pltpu.VMEM((count, message, LANES), f32),
         pltpu.VMEM((2, LANES, LANES), bf16),
         pltpu.VMEM((2, LANES, LANES), bf16),
         pltpu.VMEM((2, size, size), bf16),
@@ -382,7 +406,7 @@
         scratch_shapes=[
             pltpu.VMEM(x.shape, f32),
             pltpu.VMEM(g.shape, f32),
-            pltpu.VMEM((count, 2 * rows_hi, LANES), f32),
+            pltpu.VMEM((count, message, LANES), f32),
             pltpu.SemaphoreType.DMA((2,)),
             pltpu.SemaphoreType.DMA((count,)),
             pltpu.SemaphoreType.DMA((count,)),
@@ -402,6 +426,7 @@
         out_specs=[pl.BlockSpec(memory_space=pltpu.HBM)] * 2,
         scratch_shapes=[
             pltpu.VMEM((2 * rows, LANES), f32),
+            pltpu.VMEM((radix, LANES // 2 // radix, size), f32),
             pltpu.VMEM((own, LANES), f32),
             pltpu.SemaphoreType.DMA((2,)),
         ],

time: 14.8 us -> 14.7 us (level)
  no operation moved by 1% of the time
where the time goes in v4:
time: 14.7 us; the launch traced here: 14.5 us
  Pallas kernels  13.9 us (95%)
  between operations  0.64 us (4%)
    pallas_call x1, Pallas kernels, merged_local(): pl.pallas_call(functools.partial(exchange_kernel, plan), out_shape=shared...  12.7 us
    pallas_call x1, Pallas kernels, merged_local(): pl.pallas_call(functools.partial(finish_kernel, radix), out_shape=(pltpu....  1.24 us

profile of v4, /device:TPU:0, one launch (start us, length us, event | category | flops | bytes accessed | tf_op | source)
XLA Modules:
  0.0 14.5 jit_solution(15840612289957125791)
XLA Ops:
  0.6 12.7 %exchange.1 = (f32[16,28,128]{2,1,0:T(8,128)S(1)}, bf16[2,128,128]{2,1,0:T(8,128)(2,1)S(1)}, bf16[2,128,128]{2,1,0:T(8,128)(2,1)S(1)}, bf16[2,256,256]{2,1,0:T(8,128)(2,1)S(1)}, bf16[2,256,256]{2,1,0:T(8,128)(2,1)S(1)}) custom-call(f32[256,128]{1,0:T(8,128)} %bitcast.14, f32[56,4,8]{2,1,0:T(4,128)} %bitcast.15), custom_call_target="tpu_custom_call" | custom-call | tf_op jit(solution)/shard_map/exchange/pallas_call | solution.py:401
  13.3 1.2 %finish.1 = (f32[256,128]{1,0:T(8,128)}, f32[32,128]{1,0:T(8,128)}) custom-call(f32[16,28,128]{2,1,0:T(8,128)S(1)} %get-tuple-element.9.recv, bf16[2,128,128]{2,1,0:T(8,128)(2,1)S(1)} %get-tuple-element.10.lane_hi, bf16[2,128,128]{2,1,0:T(8,128)(2,1)S(1)} %get-tuple-element.11.lane_lo, bf16[2,256,256]{2,1,0:T(8,128)(2,1)S(1)} %get-tuple-element.12.row_hi, ...), custom_call_target="tpu_custom_call" | custom-call | tf_op jit(solution)/shard_map/finish/pallas_call | solution.py:422

commit v5 on v4

--- a/solution.py
+++ b/solution.py
@@ -145,13 +145,13 @@
         return lax.rem(w + dw, radix), lax.rem(n + dn, radix)
 
     barrier = pltpu.get_barrier_semaphore()
-    for dw, dn in offsets:
-        pw, pn = partner(dw, dn)
-        pl.semaphore_signal(barrier, inc=1, device_id={"wide": pw, "narrow": pn}, device_id_type=MESH)
     copy_g = pltpu.make_async_copy(g_hbm, g, local_sem.at[0])
     copy_x = pltpu.make_async_copy(x_hbm, x, local_sem.at[1])
     copy_g.start()
     copy_x.start()
+    for dw, dn in offsets:
+        pw, pn = partner(dw, dn)
+        pl.semaphore_signal(barrier, inc=1, device_id={"wide": pw, "narrow": pn}, device_id_type=MESH)
     copy_g.wait()
 
     planes = []
@@ -252,11 +252,11 @@
     pl.semaphore_wait(barrier, len(offsets))
     me = w * radix + n
     count = radix * radix
-    seat = n * radix + w
+    seat = ((radix - n) % radix) * radix + w
     copies = []
     for at in range(count - 1):
         other = at + (at + count - seat) // count
-        pw, pn = other % radix, other // radix
+        pw, pn = other % radix, (radix - other // radix) % radix
         copy = pltpu.make_async_remote_copy(
             src_ref=send.at[pw * radix + pn],
             dst_ref=recv.at[me],
@@ -296,7 +296,7 @@
         copy.wait_send()
     for at in range(count - 1):
         other = at + (at + count - seat) // count
-        pw, pn = other % radix, other // radix
+        pw, pn = other % radix, (radix - other // radix) % radix
         pltpu.make_async_remote_copy(
             src_ref=send.at[me],
             dst_ref=recv.at[pw * radix + pn],

time: 14.7 us -> 13.9 us (0.946)
  Pallas kernels: 13.9 us -> 13.1 us
    pallas_call x1, Pallas kernels: 12.7 us -> 11.8 us  [merged_local(): pl.pallas_call(functools.partial(exchange_kernel, plan), out_shape=shared...]
where the time goes in v5:
time: 13.9 us; the launch traced here: 13.7 us
  Pallas kernels  13.1 us (94%)
  between operations  0.64 us (5%)
    pallas_call x1, Pallas kernels, merged_local(): pl.pallas_call(functools.partial(exchange_kernel, plan), out_shape=shared...  11.8 us
    pallas_call x1, Pallas kernels, merged_local(): pl.pallas_call(functools.partial(finish_kernel, radix), out_shape=(pltpu....  1.24 us

profile of v5, /device:TPU:0, one launch (start us, length us, event | category | flops | bytes accessed | tf_op | source)
XLA Modules:
  0.0 13.7 jit_solution(366415809514730823)
XLA Ops:
  0.6 11.8 %exchange.1 = (f32[16,28,128]{2,1,0:T(8,128)S(1)}, bf16[2,128,128]{2,1,0:T(8,128)(2,1)S(1)}, bf16[2,128,128]{2,1,0:T(8,128)(2,1)S(1)}, bf16[2,256,256]{2,1,0:T(8,128)(2,1)S(1)}, bf16[2,256,256]{2,1,0:T(8,128)(2,1)S(1)}) custom-call(f32[256,128]{1,0:T(8,128)} %bitcast.14, f32[56,4,8]{2,1,0:T(4,128)} %bitcast.15), custom_call_target="tpu_custom_call" | custom-call | tf_op jit(solution)/shard_map/exchange/pallas_call | solution.py:401
  12.5 1.2 %finish.1 = (f32[256,128]{1,0:T(8,128)}, f32[32,128]{1,0:T(8,128)}) custom-call(f32[16,28,128]{2,1,0:T(8,128)S(1)} %get-tuple-element.9.recv, bf16[2,128,128]{2,1,0:T(8,128)(2,1)S(1)} %get-tuple-element.10.lane_hi, bf16[2,128,128]{2,1,0:T(8,128)(2,1)S(1)} %get-tuple-element.11.lane_lo, bf16[2,256,256]{2,1,0:T(8,128)(2,1)S(1)} %get-tuple-element.12.row_hi, ...), custom_call_target="tpu_custom_call" | custom-call | tf_op jit(solution)/shard_map/finish/pallas_call | solution.py:422
